TPU v7x, 32 devices: a whole 2x2x4 slice. The times are simulated.
32 devices in a mesh: row: 4 (over z), col: 8 (over y, x, core).
Axes of the slice: x: 2, y: 2, z: 4, core: 2. Of those that a mesh axis runs over, the one named last changes fastest.
Arguments:
- matrix: float32 [15360, 15360], P('row', 'col'), may hold values from -4 to 4
- rhs: float32 [15360, 4096], P('row', 'col'), may hold values from -6 to 6
- pivot_inverses: bfloat16 [2, 512, 512], replicated, may hold values from -0.046875 to 0.046875
- panel_order: int32 [2], replicated, may hold values from 0 to 29, as said below
Outputs:
- factored: bfloat16 [15360, 15360], P('row', 'col')
- updated_rhs: float32 [15360, 4096], P('row', 'col')
- rhs_norms: float32 [4096], P('col')
Inputs may be any that keep to these rules, and one draw needn't show every extreme that they name: `panel_order`: two different panel indices, one of which is the last panel, 29.
All inputs are finite; a program needn't handle non-finite values.
Results may differ from a plain program's by a relative error of at most 0.001.
Values sent between devices are 32-bit elements; how exact they have to be, the bound alone decides.
No kernel may reach another device: no remote copies, remote signals or barrier semaphores. Data moves between devices by JAX's collectives and lax.ppermute only.
A program may use at most 192 MiB of HBM per device.

v0:
```python
import jax
import jax.numpy as jnp
from jax import lax
from jax.sharding import PartitionSpec as P

N = 15360
PW = 512


def product(first, second):
    return jnp.dot(
        first, second, precision=lax.Precision.HIGHEST, preferred_element_type=jnp.float32
    )


def cut_along(values, start, length, axis_dim):
    return lax.dynamic_slice_in_dim(values, start, length, axis_dim)


def refresh(sub_block, mult_rows, upper_rows, row_keep, col_keep, fresh_col, placed):
    updated = sub_block - row_keep[:, None] * product(mult_rows, upper_rows * col_keep[None, :])
    return jnp.where((row_keep[:, None] > 0) & (fresh_col[None, :] > 0), placed, updated)


def on_device(matrix, rhs, pivot_inverses, panel_order):
    row_count = lax.axis_size("row")
    col_count = lax.axis_size("col")
    block_size = PW // row_count
    group_count = col_count // row_count
    col_index = lax.axis_index("col")
    row_len, col_len = matrix.shape
    row_block_id = jnp.arange(row_len, dtype=jnp.int32) // block_size
    col_block_id = jnp.arange(col_len, dtype=jnp.int32) // block_size

    def column_hit(panel_id):
        is_owner = col_index // row_count == panel_id % group_count
        return (
            ((col_block_id == panel_id // group_count) & is_owner).astype(jnp.float32),
            is_owner,
        )

    def take_slices(current, right_sides, panel_id):
        start = panel_id * block_size
        return (
            cut_along(current, start, block_size, 0),
            cut_along(right_sides, start, block_size, 0),
            cut_along(current, panel_id // group_count * block_size, block_size, 1),
        )

    current = matrix
    right_sides = rhs
    row_piece, rhs_piece, column_slab = take_slices(current, right_sides, panel_order[0])
    for section in range(2):
        panel_id = panel_order[section]
        row_keep = jnp.ones((row_len,), jnp.float32)
        col_keep = jnp.ones((col_len,), jnp.float32)
        for earlier in range(section + 1):
            row_keep = row_keep * (row_block_id != panel_order[earlier]).astype(jnp.float32)
            hit, owner_flag = column_hit(panel_order[earlier])
            col_keep = col_keep * (1.0 - hit)
        fresh_col, keep_is_owner = column_hit(panel_order[section])
        row_keep, col_keep, fresh_col, is_owner = (row_keep, col_keep, fresh_col, keep_is_owner)
        upper_rows, rhs_rows = (
            lax.all_gather(row_piece, "row", axis=0, tiled=True),
            lax.all_gather(rhs_piece, "row", axis=0, tiled=True),
        )
        inverse = pivot_inverses[section].astype(jnp.float32)
        own_rows = cut_along(inverse, col_index % row_count * block_size, block_size, 0)
        partial_value = jnp.where(is_owner, product(column_slab, own_rows), 0.0)
        multipliers = lax.psum(partial_value, "col")
        own_mult = cut_along(multipliers, col_index % row_count * block_size, block_size, 1)
        placed = lax.dynamic_update_slice_in_dim(
            jnp.zeros_like(current), own_mult, panel_id // group_count * block_size, 1
        )
        current = refresh(current, multipliers, upper_rows, row_keep, col_keep, fresh_col, placed)
        right_sides = right_sides - row_keep[:, None] * product(multipliers, rhs_rows)
        if section == 0:
            row_piece, rhs_piece, column_slab = take_slices(current, right_sides, panel_order[1])
    totals = lax.psum(jnp.sum(right_sides * right_sides, axis=0), "row")
    rhs_norms = jnp.sqrt(totals / N + 1e-06)
    return (current.astype(jnp.bfloat16), right_sides, rhs_norms)


def solution(mesh):
    in_specs = (P("row", "col"), P("row", "col"), P(), P())
    out_specs = (P("row", "col"), P("row", "col"), P("col"))
    return jax.shard_map(
        on_device, mesh=mesh, in_specs=in_specs, out_specs=out_specs, check_vma=False
    )
```

profile of v0, /device:TPU:0, one launch (start us, length us, event | category | flops | bytes accessed | tf_op | source)
XLA Modules:
  0.0 484.3 jit_solution(17791880367086263619)
XLA Ops:
  8.0 0.0 all-gather.9.cloned.1.call-start
  8.0 1.4 fusion.28
  10.1 1.7 constant_dynamic-slice_fusion.3
  11.8 0.0 all-reduce.3.cloned.1.call-start
  14.5 1.3 fusion.27
  15.7 6.9 %convolution_select_fusion.1 = f32[3840,512]{1,0:T(8,128)} fusion(pred[]{:T(512)S(6)} %eq.59, f32[3840,1920]{1,0:T(8,128)} %param.4, s32[]{:T(128)S(6)} %select_n.140, bf16[1,512,512]{2,1,0:T(8,128)(2,1)S(1)} %get-tuple-element.4, s32[]{:T(128)S(6)} %select_n.142), kind=kOutput, calls=%fused_computation.6 | convolution fusion | flops 3021864960 | bytes 9961481 | tf_op jit(solution)/shard_map/dot_general | solution.py:11
  22.7 0.0 all-gather.5.cloned.1.call-start
  22.7 2.3 constant_dynamic-slice_fusion.2
  25.0 0.0 all-gather.11.cloned.1.call-start
  28.5 0.7 broadcast_compare_fusion
  29.2 0.7 fusion.15
  29.9 12.8 %all-gather.9.cloned.1.call-done = f32[512,512]{1,0:T(8,128)} async-done(((f32[128,512]{1,0:T(8,128)}), f32[512,512]{1,0:T(8,128)}) %all-gather.9.cloned.1.call-update) | async-done | bytes 1048592 | tf_op jit(solution)/shard_map/all_gather | solution.py:65
  42.6 103.8 %all-reduce.3.cloned.1.call-done = f32[3840,512]{1,0:T(8,128)} async-done(((f32[3840,512]{1,0:T(8,128)}), f32[3840,512]{1,0:T(8,128)}) %all-reduce.3.cloned.1.call-update) | async-done | bytes 7864336 | tf_op jit(solution)/shard_map/psum | solution.py:70
  146.4 16.6 %multiply_subtract_fusion.1 = f32[3840,512]{1,0:T(8,128)S(1)} fusion(f32[3840,512]{1,0:T(8,128)} %param.5, f32[3840,512]{1,0:T(8,128)} %all-reduce.3.cloned.1.call-done, f32[512,512]{1,0:T(8,128)} %all-gather.9.cloned.1.call-done, f32[3840]{0:T(1024)S(1)} %fusion.15), kind=kOutput, calls=%fused_computation.4 | convolution fusion | flops 12083527680 | bytes 24656896 | tf_op jit(solution)/shard_map/dot_general | solution.py:11
  163.0 3.2 copy-done
  166.2 0.7 constant_dynamic-slice_fusion
  167.0 0.2 all-reduce.5.cloned.1.call-start
  167.2 11.9 %broadcast.286.clone = f32[3840,1920]{1,0:T(8,128)} broadcast(f32[]{:T(128)} %constant.140.clone.1), dimensions={} | broadcast | bytes 29491204 | tf_op jit(solution)/shard_map/broadcast.6
  179.1 3.1 dynamic-slice_dynamic-update-slice_fusion.1
  182.2 61.2 %subtract_select_fusion = f32[3840,1920]{1,0:T(8,128)} fusion(f32[3840,1920]{1,0:T(8,128)} %dynamic-slice_dynamic-update-slice_fusion.1, f32[3840,1920]{1,0:T(8,128)} %param.4, f32[3840,512]{1,0:T(8,128)} %all-reduce.3.cloned.1.call-done, f32[3840]{0:T(1024)S(1)} %fusion.15, pred[1920]{0:T(1024)(128)(4,1)S(1)} %convert_compare_fusion, ...), kind=kOutput, calls=%fused_computation.1 | convolution fusion | flops 45328957440 | bytes 100298880 | tf_op jit(solution)/shard_map/dot_general | solution.py:11
  243.4 6.9 %convolution_select_fusion = f32[3840,512]{1,0:T(8,128)} fusion(pred[]{:T(512)S(6)} %eq.56, f32[3840,1920]{1,0:T(8,128)} %subtract_select_fusion, s32[]{:T(128)S(6)} %select_n.146, bf16[1,512,512]{2,1,0:T(8,128)(2,1)S(1)} %get-tuple-element.3, s32[]{:T(128)S(6)} %select_n.142), kind=kOutput, calls=%fused_computation.5 | convolution fusion | flops 3021864960 | bytes 9961481 | tf_op jit(solution)/shard_map/dot_general | solution.py:11
  250.3 0.3 all-gather.7.cloned.1.call-start
  250.6 2.2 constant_dynamic-slice_fusion.1
  252.9 1.3 broadcast_compare_fusion.1
  254.2 1.3 fusion.14
  255.6 115.9 %all-reduce.5.cloned.1.call-done = f32[3840,512]{1,0:T(8,128)} async-done(((f32[3840,512]{1,0:T(8,128)}), f32[3840,512]{1,0:T(8,128)}) %all-reduce.5.cloned.1.call-update) | async-done | bytes 7864336 | tf_op jit(solution)/shard_map/psum | solution.py:70
  371.5 17.8 %multiply_reduce_fusion = (f32[512]{0:T(512)S(1)}, f32[3840,512]{1,0:T(8,128)}) fusion(f32[3840,512]{1,0:T(8,128)} %copy-done, f32[3840,512]{1,0:T(8,128)} %all-reduce.5.cloned.1.call-done, f32[512,512]{1,0:T(8,128)} %all-gather.11.cloned.1.call-done, f32[3840]{0:T(1024)S(1)} %fusion.14), kind=kOutput, calls=%fused_computation.2 | convolution fusion | flops 12087459840 | bytes 24658944 | tf_op jit(solution)/shard_map/dot_general | solution.py:11
  389.2 11.7 %psum.23 = f32[512]{0:T(512)S(1)} all-reduce(f32[512]{0:T(512)S(1)} %get-tuple-element.7), channel_id=1, replica_groups=mesh['row'=4,'col'=8] {'row'}, use_global_device_ids=true, to_apply=%region_3.4 | all-reduce | flops 512 | bytes 4096 | tf_op jit(solution)/shard_map/psum | solution.py:79
  400.9 0.6 add_sqrt_fusion
  401.5 11.6 %broadcast.286 = f32[3840,1920]{1,0:T(8,128)} broadcast(f32[]{:T(128)} %constant.140.clone.1), dimensions={} | broadcast | bytes 29491204 | tf_op jit(solution)/shard_map/broadcast.6
  413.1 3.1 dynamic-slice_dynamic-update-slice_fusion
  416.2 60.9 %select_convert_fusion = bf16[3840,1920]{1,0:T(8,128)(2,1)} fusion(f32[3840,1920]{1,0:T(8,128)} %dynamic-slice_dynamic-update-slice_fusion, f32[3840,1920]{1,0:T(8,128)} %subtract_select_fusion, f32[3840,512]{1,0:T(8,128)} %all-reduce.5.cloned.1.call-done, f32[3840]{0:T(1024)S(1)} %fusion.14, pred[1920]{0:T(1024)(128)(4,1)S(1)} %convert_compare_fusion.1, ...), kind=kOutput, calls=%fused_computation | convolution fusion | flops 45328957440 | bytes 85553280 | tf_op jit(solution)/shard_map/dot_general | solution.py:11
  (14 shorter events, 0.2 us)
Async XLA Ops:
  8.0 34.6 %all-gather.9.cloned.1.call-start = ((), (), s32[]{:S(2)}) async-start(), calls=%async_computation.4 | async-start | bytes 1310720 | tf_op jit(solution)/shard_map/all_gather | solution.py:65
  11.8 134.6 %all-reduce.3.cloned.1.call-start = ((), (), s32[]{:S(2)}) async-start(), calls=%async_computation | async-start | bytes 15728640 | tf_op jit(solution)/shard_map/psum | solution.py:70
  22.7 159.5 %all-gather.5.cloned.1.call-start = ((), (), s32[]{:S(2)}) async-start(), calls=%async_computation.1 | async-start | bytes 4915200 | tf_op jit(solution)/shard_map/all_gather | solution.py:64
  25.0 230.5 %all-gather.11.cloned.1.call-start = ((), (), s32[]{:S(2)}) async-start(), calls=%async_computation.5 | async-start | bytes 1310720 | tf_op jit(solution)/shard_map/all_gather | solution.py:65
  163.0 3.2 copy-start
  167.0 204.5 %all-reduce.5.cloned.1.call-start = ((), (), s32[]{:S(2)}) async-start(), calls=%async_computation.2 | async-start | bytes 15728640 | tf_op jit(solution)/shard_map/psum | solution.py:70
  250.3 165.9 %all-gather.7.cloned.1.call-start = ((), (), s32[]{:S(2)}) async-start(), calls=%async_computation.3 | async-start | bytes 4915200 | tf_op jit(solution)/shard_map/all_gather | solution.py:64
Sparse Core Ops, SparseCore 0:
  11.9 30.6 all-gather.8
  44.2 75.7 all-gather.4
  167.1 28.0 all-gather.10
  253.0 76.5 all-gather.6
Sparse Core Ops, SparseCore 1:
  22.7 123.6 all-reduce.2
  250.4 121.0 all-reduce.4
where the time goes:
time: 485 us; the launch traced here: 484 us
  waiting for transfers between devices  233 us (48%)
  matrix products  170 us (35%)
  local copies, waits for them, and re-layouts  42.5 us (9%)
  between operations  22 us (5%)
  blocking collectives  11.7 us (2%)
    psum x2, waiting for transfers between devices, on_device(): multipliers = lax.psum(partial_value, 'col')  220 us
    dot_general x6, matrix products, product(): jnp.dot(first, second, precision=lax.Precision.HIGHEST, preferred_element...  170 us
    another operation x2, local copies, waits for them, and re-layouts  23.5 us
    all_gather x2, waiting for transfers between devices, on_device(): lax.all_gather(rhs_piece, 'row', axis=0, tiled=True)  12.8 us
    psum x1, blocking collectives, on_device(): totals = lax.psum(jnp.sum(right_sides * right_sides, axis=0), 'row')  11.7 us
  transfers between devices with their start and end apart: 6, of which 3 were waited for; matrix products, arithmetic and copies ran while one was open for 31% of the time, Pallas kernels for 0%

commit v1 on v0

--- a/solution.py
+++ b/solution.py
@@ -67,7 +67,8 @@
         inverse = pivot_inverses[section].astype(jnp.float32)
         own_rows = cut_along(inverse, col_index % row_count * block_size, block_size, 0)
         partial_value = jnp.where(is_owner, product(column_slab, own_rows), 0.0)
-        multipliers = lax.psum(partial_value, "col")
+        parts = lax.all_gather(partial_value, "col")
+        multipliers = jnp.sum(parts, axis=0)
         own_mult = cut_along(multipliers, col_index % row_count * block_size, block_size, 1)
         placed = lax.dynamic_update_slice_in_dim(
             jnp.zeros_like(current), own_mult, panel_id // group_count * block_size, 1

time: 485 us -> 913 us (1.88)
  waiting for transfers between devices: 233 us -> 614 us
  other arithmetic: 4.61 us -> 52.6 us
    all_gather x0 -> x2, waiting for transfers between devices: none -> 536 us  [on_device(): parts = lax.all_gather(partial_value, 'col')]
    psum x2 -> x0, waiting for transfers between devices: 220 us -> none  [on_device(): multipliers = lax.psum(partial_value, 'col')]
    all_gather x2, waiting for transfers between devices: 0.01 us -> 72.3 us  [on_device(): lax.all_gather(row_piece, 'row', axis=0, tiled=True)]
    reduce_sum x0 -> x2, other arithmetic: none -> 48.2 us  [on_device(): multipliers = jnp.sum(parts, axis=0)]
  transfers between devices with their start and end apart: 6 -> 6, of which waited for: 3 -> 5; matrix products, arithmetic and copies ran while one was open for 31% -> 21% of each run, Pallas kernels for 0% -> 0%
where the time goes in v1:
time: 913 us; the launch traced here: 912 us
  waiting for transfers between devices  614 us (67%)
  matrix products  170 us (19%)
  other arithmetic  52.6 us (6%)
  local copies, waits for them, and re-layouts  43.7 us (5%)
  between operations  20.4 us (2%)
  blocking collectives  11 us (1%)
    all_gather x2, waiting for transfers between devices, on_device(): parts = lax.all_gather(partial_value, 'col')  536 us
    dot_general x6, matrix products, product(): jnp.dot(first, second, precision=lax.Precision.HIGHEST, preferred_element...  170 us
    all_gather x2, waiting for transfers between devices, on_device(): lax.all_gather(row_piece, 'row', axis=0, tiled=True)  72.3 us
    reduce_sum x2, other arithmetic, on_device(): multipliers = jnp.sum(parts, axis=0)  48.2 us
    another operation x2, local copies, waits for them, and re-layouts  23.5 us
  transfers between devices with their start and end apart: 6, of which 5 were waited for; matrix products, arithmetic and copies ran while one was open for 21% of the time, Pallas kernels for 0%

profile of v1, /device:TPU:0, one launch (start us, length us, event | category | flops | bytes accessed | tf_op | source)
XLA Modules:
  0.0 912.2 jit_solution(3910698292947535390)
XLA Ops:
  7.2 1.3 fusion.28
  11.2 1.3 fusion.27
  12.5 6.9 convolution_select_fusion.1
  20.1 2.2 constant_dynamic-slice_fusion.2
  22.4 1.7 constant_dynamic-slice_fusion.3
  24.1 0.2 all-gather.19.cloned.1.call-start
  24.3 0.7 fusion.15
  25.0 0.7 broadcast_compare_fusion
  27.9 279.3 %all-gather.17.cloned.1.call-done = f32[30720,512]{1,0:T(8,128)} async-done(((f32[3840,512]{1,0:T(8,128)}), f32[30720,512]{1,0:T(8,128)}) %all-gather.17.cloned.1.call-update) | async-done | bytes 62914576 | tf_op jit(solution)/shard_map/all_gather | solution.py:70
  307.2 24.5 %reduce_sum.27 = f32[3840,512]{1,0:T(8,128)} reduce(f32[8,3840,512]{2,1,0:T(8,128)} %bitcast.18, f32[]{:T(128)} %constant.140.clone.1), dimensions={0}, to_apply=%region_0.1 | reduce | flops 13762560 | bytes 70778880 | tf_op jit(solution)/shard_map/reduce_sum | solution.py:71
  331.7 11.8 %broadcast.286.clone = f32[3840,1920]{1,0:T(8,128)} broadcast(f32[]{:T(128)} %constant.140.clone.1), dimensions={} | broadcast | bytes 29491204 | tf_op jit(solution)/shard_map/broadcast.6
  343.5 3.1 dynamic-slice_dynamic-update-slice_fusion.1
  346.6 39.2 %all-gather.9.cloned.1.call-done = f32[512,1920]{1,0:T(8,128)} async-done(((f32[128,1920]{1,0:T(8,128)}), f32[512,1920]{1,0:T(8,128)}) %all-gather.9.cloned.1.call-update) | async-done | bytes 3932176 | tf_op jit(solution)/shard_map/all_gather | solution.py:64
  385.8 61.1 %subtract_select_fusion = f32[3840,1920]{1,0:T(8,128)} fusion(f32[3840,1920]{1,0:T(8,128)} %dynamic-slice_dynamic-update-slice_fusion.1, f32[3840,1920]{1,0:T(8,128)} %param.4, f32[3840,512]{1,0:T(8,128)} %reduce_sum.27, f32[3840]{0:T(1024)S(1)} %fusion.15, pred[1920]{0:T(1024)(128)(4,1)S(1)} %convert_compare_fusion, ...), kind=kOutput, calls=%fused_computation.1 | convolution fusion | flops 45328957440 | bytes 100298880 | tf_op jit(solution)/shard_map/dot_general | solution.py:11
  446.9 6.9 convolution_select_fusion
  453.9 0.3 all-gather.15.cloned.1.call-start
  454.7 16.6 %multiply_subtract_fusion.1 = f32[3840,512]{1,0:T(8,128)S(1)} fusion(f32[3840,512]{1,0:T(8,128)} %param.5, f32[3840,512]{1,0:T(8,128)} %reduce_sum.27, f32[512,512]{1,0:T(8,128)} %all-gather.13.cloned.1.call-done, f32[3840]{0:T(1024)S(1)} %fusion.15), kind=kOutput, calls=%fused_computation.4 | convolution fusion | flops 12083527680 | bytes 24656896 | tf_op jit(solution)/shard_map/dot_general | solution.py:11
  471.4 4.3 copy-done
  475.7 0.7 constant_dynamic-slice_fusion
  476.5 2.2 constant_dynamic-slice_fusion.1
  478.8 1.2 broadcast_compare_fusion.1
  480.0 1.2 fusion.14
  481.2 256.3 %all-gather.19.cloned.1.call-done = f32[30720,512]{1,0:T(8,128)} async-done(((f32[3840,512]{1,0:T(8,128)}), f32[30720,512]{1,0:T(8,128)}) %all-gather.19.cloned.1.call-update) | async-done | bytes 62914576 | tf_op jit(solution)/shard_map/all_gather | solution.py:70
  737.5 23.7 %reduce_sum.28 = f32[3840,512]{1,0:T(8,128)} reduce(f32[8,3840,512]{2,1,0:T(8,128)} %bitcast.19, f32[]{:T(128)} %constant.140.clone.1), dimensions={0}, to_apply=%region_1.2 | reduce | flops 13762560 | bytes 70778880 | tf_op jit(solution)/shard_map/reduce_sum | solution.py:71
  761.2 5.7 all-gather.15.cloned.1.call-done
  767.0 17.8 %multiply_reduce_fusion = (f32[512]{0:T(512)S(1)}, f32[3840,512]{1,0:T(8,128)}) fusion(f32[3840,512]{1,0:T(8,128)} %copy-done, f32[3840,512]{1,0:T(8,128)} %reduce_sum.28, f32[512,512]{1,0:T(8,128)} %all-gather.15.cloned.1.call-done, f32[3840]{0:T(1024)S(1)} %fusion.14), kind=kOutput, calls=%fused_computation.2 | convolution fusion | flops 12087459840 | bytes 24658944 | tf_op jit(solution)/shard_map/dot_general | solution.py:11
  784.7 11.0 %psum.7 = f32[512]{0:T(512)S(1)} all-reduce(f32[512]{0:T(512)S(1)} %get-tuple-element.7), channel_id=1, replica_groups=mesh['row'=4,'col'=8] {'row'}, use_global_device_ids=true, to_apply=%region_3.4 | all-reduce | flops 512 | bytes 4096 | tf_op jit(solution)/shard_map/psum | solution.py:80
  795.7 0.6 add_sqrt_fusion
  796.3 11.8 %broadcast.286 = f32[3840,1920]{1,0:T(8,128)} broadcast(f32[]{:T(128)} %constant.140.clone.1), dimensions={} | broadcast | bytes 29491204 | tf_op jit(solution)/shard_map/broadcast.6
  808.0 3.2 dynamic-slice_dynamic-update-slice_fusion
  811.3 33.1 %all-gather.11.cloned.1.call-done = f32[512,1920]{1,0:T(8,128)} async-done(((f32[128,1920]{1,0:T(8,128)}), f32[512,1920]{1,0:T(8,128)}) %all-gather.11.cloned.1.call-update) | async-done | bytes 3932176 | tf_op jit(solution)/shard_map/all_gather | solution.py:64
  844.4 60.9 %select_convert_fusion = bf16[3840,1920]{1,0:T(8,128)(2,1)} fusion(f32[3840,1920]{1,0:T(8,128)} %dynamic-slice_dynamic-update-slice_fusion, f32[3840,1920]{1,0:T(8,128)} %subtract_select_fusion, f32[3840,512]{1,0:T(8,128)} %reduce_sum.28, f32[3840]{0:T(1024)S(1)} %fusion.14, pred[1920]{0:T(1024)(128)(4,1)S(1)} %convert_compare_fusion.1, ...), kind=kOutput, calls=%fused_computation | convolution fusion | flops 45328957440 | bytes 85553280 | tf_op jit(solution)/shard_map/dot_general | solution.py:11
  (16 shorter events, 0.3 us)
Async XLA Ops:
  7.2 300.1 %all-gather.17.cloned.1.call-start = ((), (), s32[]{:S(2)}) async-start(), calls=%async_computation.4 | async-start | bytes 70778880 | tf_op jit(solution)/shard_map/all_gather | solution.py:70
  19.4 366.4 %all-gather.9.cloned.1.call-start = ((), (), s32[]{:S(2)}) async-start(), calls=%async_computation | async-start | bytes 4915200 | tf_op jit(solution)/shard_map/all_gather | solution.py:64
  22.3 432.4 %all-gather.13.cloned.1.call-start = ((), (), s32[]{:S(2)}) async-start(), calls=%async_computation.2 | async-start | bytes 1310720 | tf_op jit(solution)/shard_map/all_gather | solution.py:65
  24.1 713.4 %all-gather.19.cloned.1.call-start = ((), (), s32[]{:S(2)}) async-start(), calls=%async_computation.5 | async-start | bytes 70778880 | tf_op jit(solution)/shard_map/all_gather | solution.py:70
  453.9 313.1 %all-gather.15.cloned.1.call-start = ((), (), s32[]{:S(2)}) async-start(), calls=%async_computation.3 | async-start | bytes 1310720 | tf_op jit(solution)/shard_map/all_gather | solution.py:65
  471.3 4.4 copy-start
  476.5 368.0 %all-gather.11.cloned.1.call-start = ((), (), s32[]{:S(2)}) async-start(), calls=%async_computation.1 | async-start | bytes 4915200 | tf_op jit(solution)/shard_map/all_gather | solution.py:64
Sparse Core Ops, SparseCore 0:
  19.5 287.6 all-gather.16
  309.4 76.4 all-gather.8
  387.4 26.4 all-gather.12
  454.0 283.4 all-gather.18
  738.9 27.9 all-gather.14
  768.4 75.9 all-gather.10
